TPU v7x, 256 devices: a whole 4x4x8 slice. The times are simulated.
256 devices in a mesh: batch: 8 (over x, z_hi), seq: 4 (over y), mp: 8 (over z_lo, core).
Axes of the slice: x: 4, y: 4, z: 8 (z_hi: 2, z_lo: 4; z = z_hi * 4 + z_lo), core: 2. Of those that a mesh axis runs over, the one named last changes fastest.
Arguments:
- context: bfloat16 [4096, 6144], P(('batch', 'seq'), 'mp'), may hold values from -0.1875 to 0.1875
- cotangent: bfloat16 [4096, 6144], P(('batch', 'seq'), 'mp'), may hold values from -6 to 6
- out_weight: bfloat16 [6144, 6144], P(None, 'mp'), may hold values from -0.078125 to 0.078125
Outputs:
- grad_weight: float32 [6144, 6144], P(('batch', 'seq'), 'mp')
- grad_context: bfloat16 [4096, 6144], P(('batch', 'seq'), 'mp')
All inputs are finite; a program needn't handle non-finite values.
Results may differ from a plain program's by a relative error of at most 0.001.
Values may be sent and summed in bfloat16 or wider, within the bound.
No kernel may reach another device: no remote copies, remote signals or barrier semaphores. Data moves between devices by JAX's collectives and lax.ppermute only.
A program may use at most 64 MiB of HBM per device.

v0:
```python
import jax
import jax.numpy as jnp
from jax import lax
from jax.sharding import PartitionSpec as P


def joined_along(blocks, dim):
    dims = list(blocks.shape[1:])
    dims[dim] *= blocks.shape[0]
    return jnp.moveaxis(blocks, 0, dim).reshape(dims)


def copy_for_each(array, axis):
    copies = jnp.broadcast_to(array, (lax.axis_size(axis), *array.shape))
    return lax.all_to_all(copies, axis, split_axis=0, concat_axis=0, tiled=True)


def gathered_copies(array, axis, dim):
    return joined_along(copy_for_each(array, axis), dim)


def shards(context, cotangent, out_weight):
    groups = lax.axis_size(("batch", "seq"))
    members = lax.axis_size("mp")
    split_rows = lax.all_to_all(context, "mp", split_axis=0, concat_axis=1, tiled=True)
    block_rows = lax.all_to_all(
        split_rows, ("batch", "seq"), split_axis=1, concat_axis=0, tiled=True
    )
    feature_block = gathered_copies(block_rows, "mp", 0)
    all_cotangent = lax.all_gather(cotangent, ("batch", "seq"), axis=0, tiled=True)
    share = split_rows.shape[0]
    shaped_context = feature_block.reshape(members, groups, share, feature_block.shape[1])
    shaped_cotangent = all_cotangent.reshape(groups, members, share, all_cotangent.shape[1])
    grad_weight = lax.dot_general(
        shaped_context,
        shaped_cotangent,
        (((0, 1, 2), (1, 0, 2)), ((), ())),
        preferred_element_type=jnp.float32,
    )
    partial_input = lax.dot_general(
        cotangent, out_weight, (((1,), (1,)), ((), ())), preferred_element_type=jnp.float32
    )
    grad_context = lax.psum_scatter(partial_input, "mp", scatter_dimension=1, tiled=True).astype(
        jnp.bfloat16
    )
    return (grad_weight, grad_context)


def solution(mesh):
    return jax.shard_map(
        shards,
        mesh=mesh,
        in_specs=(P(("batch", "seq"), "mp"), P(("batch", "seq"), "mp"), P(None, "mp")),
        out_specs=(P(("batch", "seq"), "mp"), P(("batch", "seq"), "mp")),
        check_vma=False,
    )
```

profile of v0, /device:TPU:1, one launch (start us, length us, event | category | flops | bytes accessed | tf_op | source)
XLA Modules:
  0.0 193.0 jit_solution(11909060434958061613)
XLA Ops:
  8.0 0.0 copy-start
  8.0 0.0 reduce-scatter.2.cloned.1.call-start
  8.1 8.6 %fusion.5 = f32[128,6144]{1,0:T(8,128)} fusion(bf16[128,768]{1,0:T(8,128)(2,1)} %param.4, bf16[6144,768]{1,0:T(8,128)(2,1)} %param.5), kind=kOutput, calls=%fused_computation.3 | convolution fusion | flops 1207959552 | bytes 12779520 | tf_op jit(solution)/shard_map/dot_general | solution.py:40
  16.7 0.0 reduce-scatter.2.cloned.1.call-update
  16.7 0.0 all-gather.2.cloned.1.call-start
  16.7 0.5 all-gather.2.cloned.1.call-update
  17.3 0.0 copy-done
  17.3 13.7 %all_to_all.40 = bf16[8,16,768]{2,1,0:T(8,128)(2,1)S(1)} all-to-all(bf16[8,16,768]{2,1,0:T(8,128)(2,1)S(1)} %bitcast.17), channel_id=1, replica_groups=mesh['batch'=8,'seq'=4,'mp'=8] {'mp'}, dimensions={0} | all-to-all | bytes 393216 | tf_op jit(solution)/shard_map/all_to_all | solution.py:25
  31.0 0.1 copy.9
  31.1 0.3 all_to_all.32
  31.3 0.2 copy.10
  31.5 28.9 %all_to_all.41 = bf16[16,32,192]{2,0,1:T(8,128)(2,1)S(1)} all-to-all(bf16[16,32,192]{2,0,1:T(8,128)(2,1)S(1)} %copy.10), channel_id=1, replica_groups=mesh['batch'=8,'seq'=4,'mp'=8] {'batch','seq'}, dimensions={1} | all-to-all | bytes 393216 | tf_op jit(solution)/shard_map/all_to_all | solution.py:26
  60.4 0.1 copy.11
  60.5 0.1 broadcast_in_dim.3
  60.6 57.5 %all_to_all.42 = bf16[8,512,192]{1,2,0:T(8,128)(2,1)S(1)} all-to-all(bf16[8,512,192]{1,2,0:T(8,128)(2,1)S(1)} %broadcast_in_dim.3), channel_id=1, replica_groups=mesh['batch'=8,'seq'=4,'mp'=8] {'mp'}, dimensions={0} | all-to-all | bytes 3145728 | tf_op jit(solution)/shard_map/all_to_all | solution.py:15
  118.2 2.4 %copy.12 = bf16[8,512,192]{2,1,0:T(8,128)(2,1)} copy(bf16[8,512,192]{1,2,0:T(8,128)(2,1)S(1)} %all_to_all.42) | data formatting | bytes 3145728 | tf_op jit(solution)/shard_map/all_to_all | solution.py:15
  120.6 0.0 reduce-scatter.2.cloned.1.call-done
  120.6 1.7 convert_element_type.3
  122.3 57.6 %all-gather.2.cloned.1.call-done = bf16[4096,768]{1,0:T(8,128)(2,1)} async-done(((bf16[128,768]{1,0:T(8,128)(2,1)}), bf16[4096,768]{1,0:T(8,128)(2,1)}) %all-gather.2.cloned.1.call-update) | async-done | bytes 6291472 | tf_op jit(solution)/shard_map/all_gather | solution.py:30
  179.9 5.7 %fusion.2 = f32[192,768]{1,0:T(8,128)} fusion(bf16[8,32,16,192]{3,2,1,0:T(8,128)(2,1)} %bitcast.14, bf16[32,8,16,768]{3,2,1,0:T(8,128)(2,1)} %bitcast.18), kind=kOutput, calls=%fused_computation.2 | convolution fusion | flops 1207959552 | bytes 8454144 | tf_op jit(solution)/shard_map/dot_general | solution.py:34
Async XLA Ops:
  8.0 9.3 %copy-start = (bf16[128,768]{1,0:T(8,128)(2,1)S(1)}, bf16[128,768]{1,0:T(8,128)(2,1)}, u32[]{:S(2)}) copy-start(bf16[128,768]{1,0:T(8,128)(2,1)} %param.3) | copy-start | bytes 589828
  8.0 112.6 %reduce-scatter.2.cloned.1.call-start = ((), (), s32[]{:S(2)}) async-start(), calls=%async_computation.5 | async-start | bytes 3538944 | tf_op jit(solution)/shard_map/reduce_scatter | solution.py:43
  16.7 163.2 %all-gather.2.cloned.1.call-start = ((), (), s32[]{:S(2)}) async-start(), calls=%async_computation.4 | async-start | bytes 6488064 | tf_op jit(solution)/shard_map/all_gather | solution.py:30
Sparse Core Ops, SparseCore 0:
  16.8 84.8 reduce-scatter.1
Sparse Core Ops, SparseCore 1:
  20.6 159.2 all-gather.1
where the time goes:
time: 193 us
  blocking collectives  100 us (52%)
  waiting for transfers between devices  58.1 us (30%)
  between operations  15.5 us (8%)
  matrix products  14.3 us (7%)
  local copies, waits for them, and re-layouts  3.13 us (2%)
    all_gather x1, waiting for transfers between devices, shards(): lax.all_gather(cotangent, ('batch', 'seq'), axis=0, tiled=True)  57.6 us
    all_to_all x1, blocking collectives, copy_for_each(): return lax.all_to_all(copies, axis, split_axis=0, concat_axis=0, tiled=True)  57.5 us
    all_to_all x1, blocking collectives, shards(): lax.all_to_all(split_rows, ('batch', 'seq'), split_axis=1, concat_axis=0,...  28.9 us
    all_to_all x1, blocking collectives, shards(): lax.all_to_all(context, 'mp', split_axis=0, concat_axis=1, tiled=True)  13.7 us
    dot_general x1, matrix products, shards(): lax.dot_general(cotangent, out_weight, (((1,), (1,)), ((), ())), preferre...  8.62 us
    dot_general x1, matrix products, shards(): lax.dot_general(shaped_context, shaped_cotangent, (((0, 1, 2), (1, 0, 2))...  5.66 us
  transfers between devices with their start and end apart: 2, of which 1 were waited for; matrix products, arithmetic and copies ran while one was open for 2% of the time, Pallas kernels for 0%

commit v1 on v0

--- a/solution.py
+++ b/solution.py
@@ -27,7 +27,12 @@
         split_rows, ("batch", "seq"), split_axis=1, concat_axis=0, tiled=True
     )
     feature_block = gathered_copies(block_rows, "mp", 0)
-    all_cotangent = lax.all_gather(cotangent, ("batch", "seq"), axis=0, tiled=True)
+    all_cotangent = jnp.concatenate(
+        lax.all_to_all(
+            jnp.stack([cotangent] * lax.axis_size(("batch", "seq"))), ("batch", "seq"), 0, 0
+        ),
+        axis=0,
+    )
     share = split_rows.shape[0]
     shaped_context = feature_block.reshape(members, groups, share, feature_block.shape[1])
     shaped_cotangent = all_cotangent.reshape(groups, members, share, all_cotangent.shape[1])

time: 193 us -> 283 us (1.47); the launches traced: 193 us -> 280 us
  waiting for transfers between devices: 58.1 us -> 158 us
  blocking collectives: 100 us -> 80.8 us
  starting transfers between devices: 0.08 us -> 4.94 us
  local copies, waits for them, and re-layouts: 3.13 us -> 6.53 us
    reduce_scatter x1, waiting for transfers between devices: 0.01 us -> 106 us  [shards(): lax.psum_scatter(partial_input, 'mp', scatter_dimension=1, tiled=True)]
    all_gather x1 -> x0, waiting for transfers between devices: 57.6 us -> none  [shards(): lax.all_gather(cotangent, ('batch', 'seq'), axis=0, tiled=True)]
    all_to_all x0 -> x1, waiting for transfers between devices: none -> 51.7 us  [shards(): lax.all_to_all(jnp.stack([cotangent] * lax.axis_size(('batch', 'seq'))),...]
    all_to_all x1, blocking collectives: 57.5 us -> 43.8 us  [copy_for_each(): return lax.all_to_all(copies, axis, split_axis=0, concat_axis=0, tiled=True)]
    all_to_all x1, blocking collectives: 28.9 us -> 22.9 us  [shards(): lax.all_to_all(split_rows, ('batch', 'seq'), split_axis=1, concat_axis=0,...]
    all_to_all x0 -> x1, starting transfers between devices: none -> 4.89 us  [shards(): lax.all_to_all(jnp.stack([cotangent] * lax.axis_size(('batch', 'seq'))),...]
    another operation x0 -> x1, local copies, waits for them, and re-layouts: none -> 3.37 us  [shards(): jnp.stack([cotangent] * lax.axis_size(('batch', 'seq')))]
  transfers between devices with their start and end apart: 2 -> 2, of which waited for: 1 -> 2; matrix products, arithmetic and copies ran while one was open for 2% -> 4% of each run, Pallas kernels for 0% -> 0%
where the time goes in v1:
time: 283 us; the launch traced here: 280 us
  waiting for transfers between devices  158 us (56%)
  blocking collectives  80.8 us (29%)
  matrix products  14.1 us (5%)
  between operations  14.1 us (5%)
  local copies, waits for them, and re-layouts  6.53 us (2%)
  starting transfers between devices  4.94 us (2%)
    reduce_scatter x1, waiting for transfers between devices, shards(): lax.psum_scatter(partial_input, 'mp', scatter_dimension=1, tiled=True)  106 us
    all_to_all x1, waiting for transfers between devices, shards(): lax.all_to_all(jnp.stack([cotangent] * lax.axis_size(('batch', 'seq'))),...  51.7 us
    all_to_all x1, blocking collectives, copy_for_each(): return lax.all_to_all(copies, axis, split_axis=0, concat_axis=0, tiled=True)  43.8 us
    all_to_all x1, blocking collectives, shards(): lax.all_to_all(split_rows, ('batch', 'seq'), split_axis=1, concat_axis=0,...  22.9 us
    all_to_all x1, blocking collectives, shards(): lax.all_to_all(context, 'mp', split_axis=0, concat_axis=1, tiled=True)  14.1 us
    dot_general x1, matrix products, shards(): lax.dot_general(cotangent, out_weight, (((1,), (1,)), ((), ())), preferre...  8.41 us
  transfers between devices with their start and end apart: 2, of which 2 were waited for; matrix products, arithmetic and copies ran while one was open for 4% of the time, Pallas kernels for 0%

profile of v1, /device:TPU:1, one launch (start us, length us, event | category | flops | bytes accessed | tf_op | source)
XLA Modules:
  0.0 279.8 jit_solution(12579087317526395054)
XLA Ops:
  7.2 0.0 copy-start
  7.2 14.1 %all_to_all.45 = bf16[8,16,768]{2,1,0:T(8,128)(2,1)S(1)} all-to-all(bf16[8,16,768]{2,1,0:T(8,128)(2,1)} %bitcast.17), channel_id=1, replica_groups=mesh['batch'=8,'seq'=4,'mp'=8] {'mp'}, dimensions={0} | all-to-all | bytes 393216 | tf_op jit(solution)/shard_map/all_to_all | solution.py:25
  21.2 0.1 copy.12
  21.3 0.3 all_to_all.35
  21.6 0.2 copy.13
  21.7 22.9 %all_to_all.46 = bf16[16,32,192]{2,0,1:T(8,128)(2,1)S(1)} all-to-all(bf16[16,32,192]{2,0,1:T(8,128)(2,1)S(1)} %copy.13), channel_id=1, replica_groups=mesh['batch'=8,'seq'=4,'mp'=8] {'batch','seq'}, dimensions={1} | all-to-all | bytes 393216 | tf_op jit(solution)/shard_map/all_to_all | solution.py:26
  44.7 0.1 copy.14
  44.8 0.1 broadcast_in_dim.3
  44.9 43.8 %all_to_all.47 = bf16[8,512,192]{1,2,0:T(8,128)(2,1)S(1)} all-to-all(bf16[8,512,192]{1,2,0:T(8,128)(2,1)S(1)} %broadcast_in_dim.3), channel_id=1, replica_groups=mesh['batch'=8,'seq'=4,'mp'=8] {'mp'}, dimensions={0} | all-to-all | bytes 3145728 | tf_op jit(solution)/shard_map/all_to_all | solution.py:15
  88.7 0.0 copy-done
  88.7 3.4 %stack.2 = bf16[32,128,768]{2,1,0:T(8,128)(2,1)} broadcast(bf16[128,768]{1,0:T(8,128)(2,1)S(1)} %copy-done), dimensions={1,2} | broadcast | bytes 6488064 | tf_op jit(solution)/shard_map/stack | solution.py:32
  92.1 4.9 %all-to-all-start.3 = ((bf16[32,128,768]{2,1,0:T(8,128)(2,1)}), bf16[32,128,768]{2,1,0:T(8,128)(2,1)}, u32[]{:S(2)}, u32[]{:S(2)}) async-start(bf16[32,128,768]{2,1,0:T(8,128)(2,1)} %stack.2), calls=%async_computation.3 | async-start | bytes 12582912 | tf_op jit(solution)/shard_map/all_to_all | solution.py:31
  97.0 0.0 reduce-scatter.2.cloned.1.call-start
  97.0 8.4 %fusion.5 = f32[128,6144]{1,0:T(8,128)} fusion(bf16[128,768]{1,0:T(8,128)(2,1)S(1)} %copy-done, bf16[6144,768]{1,0:T(8,128)(2,1)} %param.5), kind=kOutput, calls=%fused_computation.3 | convolution fusion | flops 1207959552 | bytes 12779520 | tf_op jit(solution)/shard_map/dot_general | solution.py:45
  105.5 0.0 reduce-scatter.2.cloned.1.call-update
  105.5 2.4 copy.15
  107.9 106.0 %reduce-scatter.2.cloned.1.call-done = f32[128,768]{1,0:T(8,128)} async-done(((f32[128,6144]{1,0:T(8,128)}), f32[128,768]{1,0:T(8,128)}) %reduce-scatter.2.cloned.1.call-update) | async-done | bytes 393232 | tf_op jit(solution)/shard_map/reduce_scatter | solution.py:48
  213.9 1.7 convert_element_type.3
  215.6 51.7 %all-to-all-done.3 = bf16[32,128,768]{2,1,0:T(8,128)(2,1)} async-done(((bf16[32,128,768]{2,1,0:T(8,128)(2,1)}), bf16[32,128,768]{2,1,0:T(8,128)(2,1)}, u32[]{:S(2)}, u32[]{:S(2)}) %all-to-all-start.3) | async-done | bytes 6291488 | tf_op jit(solution)/shard_map/all_to_all | solution.py:31
  267.3 5.7 %fusion.2 = f32[192,768]{1,0:T(8,128)} fusion(bf16[8,32,16,192]{3,2,1,0:T(8,128)(2,1)} %bitcast.14, bf16[32,8,16,768]{3,2,1,0:T(8,128)(2,1)} %bitcast.5), kind=kOutput, calls=%fused_computation.2 | convolution fusion | flops 1207959552 | bytes 8454144 | tf_op jit(solution)/shard_map/dot_general | solution.py:39
Async XLA Ops:
  7.2 81.6 %copy-start = (bf16[128,768]{1,0:T(8,128)(2,1)S(1)}, bf16[128,768]{1,0:T(8,128)(2,1)}, u32[]{:S(2)}) copy-start(bf16[128,768]{1,0:T(8,128)(2,1)} %param.4) | copy-start | bytes 589828
  92.1 175.2 %all-to-all-start.3 = ((bf16[32,128,768]{2,1,0:T(8,128)(2,1)}), bf16[32,128,768]{2,1,0:T(8,128)(2,1)}, u32[]{:S(2)}, u32[]{:S(2)}) async-start(bf16[32,128,768]{2,1,0:T(8,128)(2,1)} %stack.2), calls=%async_computation.3 | async-start | bytes 12582912 | tf_op jit(solution)/shard_map/all_to_all | solution.py:31
  97.0 116.9 %reduce-scatter.2.cloned.1.call-start = ((), (), s32[]{:S(2)}) async-start(), calls=%async_computation.5 | async-start | bytes 3538944 | tf_op jit(solution)/shard_map/reduce_scatter | solution.py:48
Sparse Core Ops, SparseCore 0:
  105.6 108.2 reduce-scatter.1
